TPU v7x, 32 devices: a whole 2x2x4 slice. The times are simulated.
32 devices in a mesh: replica: 8 (over z, x), model: 4 (over y, core).
Axes of the slice: x: 2, y: 2, z: 4, core: 2. Of those that a mesh axis runs over, the one named last changes fastest.
Arguments:
- grad_up: float32 [8, 1280, 5120], P('replica', None, 'model'), may hold values from -4 to 4
- grad_down: float32 [8, 5120, 1280], P('replica', 'model'), may hold values from -4 to 4
- grad_query: float32 [8, 1280, 1280], P('replica', None, 'model'), may hold values from -4 to 4
- grad_key: float32 [8, 1280, 1280], P('replica', None, 'model'), may hold values from -4 to 4
- grad_value: float32 [8, 1280, 1280], P('replica', None, 'model'), may hold values from -4 to 4
- grad_mixed: float32 [8, 1280, 1280], P('replica', 'model'), may hold values from -4 to 4
- grad_norm: float32 [8, 1280], P('replica'), may hold values from -8 to 8
- weight_up: float32 [1280, 5120], P('replica', 'model'), may hold values from -0.15625 to 0.15625
- weight_down: float32 [5120, 1280], P('model', 'replica'), may hold values from -0.078125 to 0.078125
- weight_query: float32 [1280, 1280], P('replica', 'model'), may hold values from -0.15625 to 0.15625
- weight_key: float32 [1280, 1280], P('replica', 'model'), may hold values from -0.15625 to 0.15625
- weight_value: float32 [1280, 1280], P('replica', 'model'), may hold values from -0.15625 to 0.15625
- weight_mixed: float32 [1280, 1280], P('model', 'replica'), may hold values from -0.15625 to 0.15625
- weight_norm: float32 [1280], P('replica'), may hold values from 0.25 to 1.75
- moment_up: float32 [1280, 5120], P('replica', 'model'), may hold values from 0.05 to 0.8
- moment_down: float32 [5120, 1280], P('model', 'replica'), may hold values from 0.05 to 0.8
- moment_query: float32 [1280, 1280], P('replica', 'model'), may hold values from 0.05 to 0.8
- moment_key: float32 [1280, 1280], P('replica', 'model'), may hold values from 0.05 to 0.8
- moment_value: float32 [1280, 1280], P('replica', 'model'), may hold values from 0.05 to 0.8
- moment_mixed: float32 [1280, 1280], P('model', 'replica'), may hold values from 0.05 to 0.8
- moment_norm: float32 [1280], P('replica'), may hold values from 0.05 to 0.8
Outputs:
- copy_up: bfloat16 [1280, 5120], P(None, 'model')
- copy_down: bfloat16 [5120, 1280], P('model')
- copy_query: bfloat16 [1280, 1280], P(None, 'model')
- copy_key: bfloat16 [1280, 1280], P(None, 'model')
- copy_value: bfloat16 [1280, 1280], P(None, 'model')
- copy_mixed: bfloat16 [1280, 1280], P('model')
- copy_norm: bfloat16 [1280], replicated
- new_up: float32 [1280, 5120], P('replica', 'model')
- new_down: float32 [5120, 1280], P('model', 'replica')
- new_query: float32 [1280, 1280], P('replica', 'model')
- new_key: float32 [1280, 1280], P('replica', 'model')
- new_value: float32 [1280, 1280], P('replica', 'model')
- new_mixed: float32 [1280, 1280], P('model', 'replica')
- new_norm: float32 [1280], P('replica')
- state_new_up: float32 [1280, 5120], P('replica', 'model')
- state_new_down: float32 [5120, 1280], P('model', 'replica')
- state_new_query: float32 [1280, 1280], P('replica', 'model')
- state_new_key: float32 [1280, 1280], P('replica', 'model')
- state_new_value: float32 [1280, 1280], P('replica', 'model')
- state_new_mixed: float32 [1280, 1280], P('model', 'replica')
- state_new_norm: float32 [1280], P('replica')
All inputs are finite; a program needn't handle non-finite values.
Results may differ from a plain program's by a relative error of at most 0.0004.
Values may be sent and summed in bfloat16 or wider, within the bound.
A program may use at most 128 MiB of HBM per device.

v0:
```python
import jax
import jax.numpy as jnp
from jax import lax
from jax.sharding import PartitionSpec as P

learn_rate = 0.05
hold_rate = 0.9


def per_device(
    grad_up,
    grad_down,
    grad_query,
    grad_key,
    grad_value,
    grad_mixed,
    grad_norm,
    weight_up,
    weight_down,
    weight_query,
    weight_key,
    weight_value,
    weight_mixed,
    weight_norm,
    moment_up,
    moment_down,
    moment_query,
    moment_key,
    moment_value,
    moment_mixed,
    moment_norm,
):
    mean_up, mean_down, mean_query, mean_key, mean_value, mean_mixed = (
        lax.psum_scatter(
            grad_up[0].astype(jnp.float32), "replica", scatter_dimension=0, tiled=True
        ),
        lax.psum_scatter(
            grad_down[0].astype(jnp.float32), "replica", scatter_dimension=1, tiled=True
        ),
        lax.psum_scatter(
            grad_query[0].astype(jnp.float32), "replica", scatter_dimension=0, tiled=True
        ),
        lax.psum_scatter(
            grad_key[0].astype(jnp.float32), "replica", scatter_dimension=0, tiled=True
        ),
        lax.psum_scatter(
            grad_value[0].astype(jnp.float32), "replica", scatter_dimension=0, tiled=True
        ),
        lax.psum_scatter(
            grad_mixed[0].astype(jnp.float32), "replica", scatter_dimension=1, tiled=True
        ),
    )
    whole_norm = lax.psum(grad_norm[0].astype(jnp.float32), "replica")
    place = lax.axis_index("replica")
    mean_norm = lax.dynamic_slice_in_dim(
        whole_norm, place * weight_norm.shape[0], weight_norm.shape[0]
    )
    mean_rate = lax.axis_size("replica") ** (-0.5)
    mean_up = mean_up * mean_rate
    mean_down = mean_down * mean_rate
    mean_query = mean_query * mean_rate
    mean_key = mean_key * mean_rate
    mean_value = mean_value * mean_rate
    mean_mixed = mean_mixed * mean_rate
    mean_norm = mean_norm * mean_rate
    state_new_up = hold_rate * moment_up + (1.0 - hold_rate) * mean_up * mean_up
    new_up = weight_up - learn_rate * mean_up * lax.rsqrt(state_new_up + 1e-06)
    state_new_down = hold_rate * moment_down + (1.0 - hold_rate) * mean_down * mean_down
    new_down = weight_down - learn_rate * mean_down * lax.rsqrt(state_new_down + 1e-06)
    state_new_query = hold_rate * moment_query + (1.0 - hold_rate) * mean_query * mean_query
    new_query = weight_query - learn_rate * mean_query * lax.rsqrt(state_new_query + 1e-06)
    state_new_key = hold_rate * moment_key + (1.0 - hold_rate) * mean_key * mean_key
    new_key = weight_key - learn_rate * mean_key * lax.rsqrt(state_new_key + 1e-06)
    state_new_value = hold_rate * moment_value + (1.0 - hold_rate) * mean_value * mean_value
    new_value = weight_value - learn_rate * mean_value * lax.rsqrt(state_new_value + 1e-06)
    state_new_mixed = hold_rate * moment_mixed + (1.0 - hold_rate) * mean_mixed * mean_mixed
    new_mixed = weight_mixed - learn_rate * mean_mixed * lax.rsqrt(state_new_mixed + 1e-06)
    state_new_norm = hold_rate * moment_norm + (1.0 - hold_rate) * mean_norm * mean_norm
    new_norm = weight_norm - learn_rate * mean_norm * lax.rsqrt(state_new_norm + 1e-06)
    copy_up, copy_down, copy_query, copy_key, copy_value, copy_mixed, copy_norm = (
        lax.all_gather(new_up.astype(jnp.bfloat16), "replica", axis=0, tiled=True),
        lax.all_gather(new_down.astype(jnp.bfloat16), "replica", axis=1, tiled=True),
        lax.all_gather(new_query.astype(jnp.bfloat16), "replica", axis=0, tiled=True),
        lax.all_gather(new_key.astype(jnp.bfloat16), "replica", axis=0, tiled=True),
        lax.all_gather(new_value.astype(jnp.bfloat16), "replica", axis=0, tiled=True),
        lax.all_gather(new_mixed.astype(jnp.bfloat16), "replica", axis=1, tiled=True),
        lax.all_gather(new_norm.astype(jnp.bfloat16), "replica", axis=0, tiled=True),
    )
    return (
        copy_up,
        copy_down,
        copy_query,
        copy_key,
        copy_value,
        copy_mixed,
        copy_norm,
        new_up,
        new_down,
        new_query,
        new_key,
        new_value,
        new_mixed,
        new_norm,
        state_new_up,
        state_new_down,
        state_new_query,
        state_new_key,
        state_new_value,
        state_new_mixed,
        state_new_norm,
    )


def solution(mesh):
    placed = (
        P("replica", None, "model"),
        P("replica", "model", None),
        P("replica", None, "model"),
        P("replica", None, "model"),
        P("replica", None, "model"),
        P("replica", "model", None),
        P("replica", None),
        P("replica", "model"),
        P("model", "replica"),
        P("replica", "model"),
        P("replica", "model"),
        P("replica", "model"),
        P("model", "replica"),
        P("replica"),
        P("replica", "model"),
        P("model", "replica"),
        P("replica", "model"),
        P("replica", "model"),
        P("replica", "model"),
        P("model", "replica"),
        P("replica"),
    )
    return jax.shard_map(
        per_device,
        mesh=mesh,
        in_specs=placed,
        out_specs=(
            P(None, "model"),
            P("model", None),
            P(None, "model"),
            P(None, "model"),
            P(None, "model"),
            P("model", None),
            P(),
            P("replica", "model"),
            P("model", "replica"),
            P("replica", "model"),
            P("replica", "model"),
            P("replica", "model"),
            P("model", "replica"),
            P("replica"),
            P("replica", "model"),
            P("model", "replica"),
            P("replica", "model"),
            P("replica", "model"),
            P("replica", "model"),
            P("model", "replica"),
            P("replica"),
        ),
        check_vma=False,
    )
```

profile of v0, /device:TPU:0, one launch (start us, length us, event | category | flops | bytes accessed | tf_op | source)
XLA Modules:
  0.0 700.8 jit_solution(5134886001297537778)
XLA Ops:
  8.0 8.2 %copy.42 = f32[1,1280,1280]{1,2,0:T(8,128)} copy(f32[1,1280,1280]{2,1,0:T(8,128)} %param.22) | data formatting | bytes 13107200 | tf_op args[1]
  19.4 1.8 copy.44
  23.1 1.8 copy.46
  25.0 111.1 %reduce-scatter.7.cloned.1.call-done = f32[160,1280]{1,0:T(8,128)} async-done(((f32[1280,1280]{1,0:T(8,128)}), f32[160,1280]{1,0:T(8,128)}) %reduce-scatter.7.cloned.1.call-update) | async-done | bytes 819216 | tf_op jit(solution)/shard_map/reduce_scatter | solution.py:34
  136.1 2.7 fusion.6
  139.0 121.7 %reduce-scatter.9.cloned.1.call-done = f32[1280,160]{0,1:T(8,128)} async-done(((f32[1280,1280]{0,1:T(8,128)}), f32[1280,160]{0,1:T(8,128)}) %reduce-scatter.9.cloned.1.call-update) | async-done | bytes 819216 | tf_op jit(solution)/shard_map/reduce_scatter | solution.py:37
  260.7 2.7 fusion.5
  264.7 20.7 %psum.7 = f32[1280]{0:T(1024)S(1)} all-reduce(f32[1280]{0:T(1024)S(1)} %reduce), channel_id=1, replica_groups=mesh['replica'=8,'model'=4] {'replica'}, use_global_device_ids=true, to_apply=%region_6.0 | all-reduce | flops 1280 | bytes 10240 | tf_op jit(solution)/shard_map/psum | solution.py:53
  286.3 17.8 %all-reduce = bf16[1280]{0:T(1024)(128)(2,1)} all-reduce(bf16[1280]{0:T(1024)(128)(2,1)S(1)} %dynamic-update-slice), channel_id=1, replica_groups=mesh['replica'=8,'model'=4] {'replica'}, use_global_device_ids=true, to_apply=%add | all-reduce | flops 1280 | bytes 5120
  304.1 28.4 %reduce-scatter.11.cloned.1.call-done = f32[160,320]{1,0:T(8,128)} async-done(((f32[1280,320]{1,0:T(8,128)}), f32[160,320]{1,0:T(8,128)}) %reduce-scatter.11.cloned.1.call-update) | async-done | bytes 204816 | tf_op jit(solution)/shard_map/reduce_scatter | solution.py:40
  332.6 1.8 fusion.4
  334.4 35.3 %all_gather.23 = bf16[1280,320]{1,0:T(8,128)(2,1)S(1)} all-gather(bf16[160,320]{1,0:T(8,128)(2,1)S(1)} %get-tuple-element.54), channel_id=1, replica_groups=mesh['replica'=8,'model'=4] {'replica'}, dimensions={0}, use_global_device_ids=true | all-gather | bytes 921600 | tf_op jit(solution)/shard_map/all_gather | solution.py:83
  370.9 36.4 %reduce-scatter.13.cloned.1.call-done = f32[160,320]{1,0:T(8,128)} async-done(((f32[1280,320]{1,0:T(8,128)}), f32[160,320]{1,0:T(8,128)}) %reduce-scatter.13.cloned.1.call-update) | async-done | bytes 204816 | tf_op jit(solution)/shard_map/reduce_scatter | solution.py:43
  407.4 1.8 fusion.3
  409.2 35.3 %all_gather.24 = bf16[1280,320]{1,0:T(8,128)(2,1)S(1)} all-gather(bf16[160,320]{1,0:T(8,128)(2,1)S(1)} %get-tuple-element.51), channel_id=1, replica_groups=mesh['replica'=8,'model'=4] {'replica'}, dimensions={0}, use_global_device_ids=true | all-gather | bytes 921600 | tf_op jit(solution)/shard_map/all_gather | solution.py:84
  445.7 35.4 %reduce-scatter.15.cloned.1.call-done = f32[160,320]{1,0:T(8,128)} async-done(((f32[1280,320]{1,0:T(8,128)}), f32[160,320]{1,0:T(8,128)}) %reduce-scatter.15.cloned.1.call-update) | async-done | bytes 204816 | tf_op jit(solution)/shard_map/reduce_scatter | solution.py:46
  481.1 1.8 fusion.2
  482.9 35.6 %all_gather.25 = bf16[1280,320]{1,0:T(8,128)(2,1)S(1)} all-gather(bf16[160,320]{1,0:T(8,128)(2,1)S(1)} %get-tuple-element.48), channel_id=1, replica_groups=mesh['replica'=8,'model'=4] {'replica'}, dimensions={0}, use_global_device_ids=true | all-gather | bytes 921600 | tf_op jit(solution)/shard_map/all_gather | solution.py:85
  519.8 35.4 %reduce-scatter.17.cloned.1.call-done = f32[320,160]{0,1:T(8,128)} async-done(((f32[320,1280]{0,1:T(8,128)}), f32[320,160]{0,1:T(8,128)}) %reduce-scatter.17.cloned.1.call-update) | async-done | bytes 204816 | tf_op jit(solution)/shard_map/reduce_scatter | solution.py:49
  555.2 1.8 fusion.1
  557.0 34.9 %all_gather.26 = bf16[320,1280]{0,1:T(8,128)(2,1)S(1)} all-gather(bf16[320,160]{0,1:T(8,128)(2,1)S(1)} %get-tuple-element.45), channel_id=1, replica_groups=mesh['replica'=8,'model'=4] {'replica'}, dimensions={1}, use_global_device_ids=true | all-gather | bytes 921600 | tf_op jit(solution)/shard_map/all_gather | solution.py:86
  593.2 30.6 %all-gather.3.cloned.1.call-done = bf16[1280,1280]{1,0:T(8,128)(2,1)} async-done(((bf16[160,1280]{1,0:T(8,128)(2,1)}), bf16[1280,1280]{1,0:T(8,128)(2,1)}) %all-gather.3.cloned.1.call-update) | async-done | bytes 3276816 | tf_op jit(solution)/shard_map/all_gather | solution.py:81
  623.8 62.8 %all-gather.5.cloned.1.call-done = bf16[1280,1280]{0,1:T(8,128)(2,1)} async-done(((bf16[1280,160]{0,1:T(8,128)(2,1)}), bf16[1280,1280]{0,1:T(8,128)(2,1)}) %all-gather.5.cloned.1.call-update) | async-done | bytes 3276816 | tf_op jit(solution)/shard_map/all_gather | solution.py:82
  686.6 5.6 copy.47
  (70 shorter events, 14.3 us)
Async XLA Ops:
  7.2 128.9 %reduce-scatter.7.cloned.1.call-start = ((), (), s32[]{:S(2)}) async-start(), calls=%async_computation.6 | async-start | bytes 7372800 | tf_op jit(solution)/shard_map/reduce_scatter | solution.py:34
  7.9 252.7 %reduce-scatter.9.cloned.1.call-start = ((), (), s32[]{:S(2)}) async-start(), calls=%async_computation.8 | async-start | bytes 7372800 | tf_op jit(solution)/shard_map/reduce_scatter | solution.py:37
  16.2 316.4 %reduce-scatter.11.cloned.1.call-start = ((), (), s32[]{:S(2)}) async-start(), calls=%async_computation.10 | async-start | bytes 2211840 | tf_op jit(solution)/shard_map/reduce_scatter | solution.py:40
  19.3 388.0 %reduce-scatter.13.cloned.1.call-start = ((), (), s32[]{:S(2)}) async-start(), calls=%async_computation.11 | async-start | bytes 2211840 | tf_op jit(solution)/shard_map/reduce_scatter | solution.py:43
  21.2 459.9 %reduce-scatter.15.cloned.1.call-start = ((), (), s32[]{:S(2)}) async-start(), calls=%async_computation.12 | async-start | bytes 2211840 | tf_op jit(solution)/shard_map/reduce_scatter | solution.py:46
  23.0 113.1 %copy-start.5 = (f32[160,1280]{1,0:T(8,128)S(1)}, f32[160,1280]{1,0:T(8,128)}, u32[]{:S(2)}) copy-start(f32[160,1280]{1,0:T(8,128)} %param.28) | copy-start | bytes 2457604
  23.0 113.0 %copy-start.6 = (f32[160,1280]{1,0:T(8,128)S(1)}, f32[160,1280]{1,0:T(8,128)}, u32[]{:S(2)}) copy-start(f32[160,1280]{1,0:T(8,128)} %param.35) | copy-start | bytes 2457604
  23.1 532.2 %reduce-scatter.17.cloned.1.call-start = ((), (), s32[]{:S(2)}) async-start(), calls=%async_computation.13 | async-start | bytes 2211840 | tf_op jit(solution)/shard_map/reduce_scatter | solution.py:49
  24.9 235.7 %copy-start.7 = (f32[1280,160]{0,1:T(8,128)S(1)}, f32[1280,160]{0,1:T(8,128)}, u32[]{:S(2)}) copy-start(f32[1280,160]{0,1:T(8,128)} %param.29) | copy-start | bytes 2457604
  25.0 235.7 %copy-start.8 = (f32[1280,160]{0,1:T(8,128)S(1)}, f32[1280,160]{0,1:T(8,128)}, u32[]{:S(2)}) copy-start(f32[1280,160]{0,1:T(8,128)} %param.36) | copy-start | bytes 2457604
  25.0 598.8 %all-gather.3.cloned.1.call-start = ((), (), s32[]{:S(2)}) async-start(), calls=%async_computation.7 | async-start | bytes 3686400 | tf_op jit(solution)/shard_map/all_gather | solution.py:81
  138.8 124.6 %copy-start.17 = (f32[1,1280]{1,0:T(1,128)S(1)}, f32[1,1280]{1,0:T(1,128)}, u32[]{:S(2)}) copy-start(f32[1,1280]{1,0:T(1,128)} %param.27) | copy-start | bytes 15364
  138.8 124.6 %copy-start.20 = (u32[32]{0:T(128)S(1)}, u32[32]{0:T(128)}, u32[]{:S(2)}) copy-start(u32[32]{0:T(128)} %constant.65) | copy-start | bytes 388
  138.9 146.6 %copy-start.18 = (f32[160]{0:T(256)S(1)}, f32[160]{0:T(256)}, u32[]{:S(2)}) copy-start(f32[160]{0:T(256)} %param.34) | copy-start | bytes 1924
  138.9 146.6 %copy-start.19 = (f32[160]{0:T(256)S(1)}, f32[160]{0:T(256)}, u32[]{:S(2)}) copy-start(f32[160]{0:T(256)} %param.41) | copy-start | bytes 1924
  138.9 193.7 %copy-start.9 = (f32[160,320]{1,0:T(8,128)S(1)}, f32[160,320]{1,0:T(8,128)}, u32[]{:S(2)}) copy-start(f32[160,320]{1,0:T(8,128)} %param.30) | copy-start | bytes 614404
  138.9 193.7 %copy-start.10 = (f32[160,320]{1,0:T(8,128)S(1)}, f32[160,320]{1,0:T(8,128)}, u32[]{:S(2)}) copy-start(f32[160,320]{1,0:T(8,128)} %param.37) | copy-start | bytes 614404
  138.9 547.7 %all-gather.5.cloned.1.call-start = ((), (), s32[]{:S(2)}) async-start(), calls=%async_computation.9 | async-start | bytes 3686400 | tf_op jit(solution)/shard_map/all_gather | solution.py:82
  304.1 103.3 %copy-start.11 = (f32[160,320]{1,0:T(8,128)S(1)}, f32[160,320]{1,0:T(8,128)}, u32[]{:S(2)}) copy-start(f32[160,320]{1,0:T(8,128)} %param.31) | copy-start | bytes 614404
  304.1 103.3 %copy-start.12 = (f32[160,320]{1,0:T(8,128)S(1)}, f32[160,320]{1,0:T(8,128)}, u32[]{:S(2)}) copy-start(f32[160,320]{1,0:T(8,128)} %param.38) | copy-start | bytes 614404
  370.9 110.1 %copy-start.13 = (f32[160,320]{1,0:T(8,128)S(1)}, f32[160,320]{1,0:T(8,128)}, u32[]{:S(2)}) copy-start(f32[160,320]{1,0:T(8,128)} %param.32) | copy-start | bytes 614404
  370.9 110.1 %copy-start.14 = (f32[160,320]{1,0:T(8,128)S(1)}, f32[160,320]{1,0:T(8,128)}, u32[]{:S(2)}) copy-start(f32[160,320]{1,0:T(8,128)} %param.39) | copy-start | bytes 614404
  445.7 109.5 %copy-start.15 = (f32[320,160]{0,1:T(8,128)S(1)}, f32[320,160]{0,1:T(8,128)}, u32[]{:S(2)}) copy-start(f32[320,160]{0,1:T(8,128)} %param.33) | copy-start | bytes 614404
  445.7 109.5 %copy-start.16 = (f32[320,160]{0,1:T(8,128)S(1)}, f32[320,160]{0,1:T(8,128)}, u32[]{:S(2)}) copy-start(f32[320,160]{0,1:T(8,128)} %param.40) | copy-start | bytes 614404
  (5 other events, 77.0 us)
Sparse Core Ops, SparseCore 0:
  11.6 124.4 reduce-scatter.6
  139.7 120.9 reduce-scatter.8
  264.7 67.8 reduce-scatter.10
  336.5 70.8 reduce-scatter.12
  410.7 70.3 reduce-scatter.14
  484.4 70.7 reduce-scatter.16
  557.4 66.3 all-gather.2
  625.9 60.6 all-gather.4
where the time goes:
time: 701 us
  waiting for transfers between devices  463 us (66%)
  blocking collectives  180 us (26%)
  local copies, waits for them, and re-layouts  29.9 us (4%)
  between operations  15 us (2%)
  other arithmetic  13.4 us (2%)
    reduce_scatter x1, waiting for transfers between devices, per_device(): lax.psum_scatter(grad_down[0].astype(jnp.float32), 'replica', scatter_dim...  122 us
    reduce_scatter x1, waiting for transfers between devices, per_device(): lax.psum_scatter(grad_up[0].astype(jnp.float32), 'replica', scatter_dimen...  111 us
    all_gather x1, waiting for transfers between devices, per_device(): lax.all_gather(new_down.astype(jnp.bfloat16), 'replica', axis=1, tiled=True)  62.8 us
    reduce_scatter x1, waiting for transfers between devices, per_device(): lax.psum_scatter(grad_key[0].astype(jnp.float32), 'replica', scatter_dime...  36.4 us
    all_gather x1, blocking collectives, per_device(): lax.all_gather(new_value.astype(jnp.bfloat16), 'replica', axis=0, tiled=T...  35.6 us
    reduce_scatter x1, waiting for transfers between devices, per_device(): lax.psum_scatter(grad_mixed[0].astype(jnp.float32), 'replica', scatter_di...  35.4 us
    reduce_scatter x1, waiting for transfers between devices, per_device(): lax.psum_scatter(grad_value[0].astype(jnp.float32), 'replica', scatter_di...  35.4 us
    all_gather x1, blocking collectives, per_device(): lax.all_gather(new_query.astype(jnp.bfloat16), 'replica', axis=0, tiled=T...  35.3 us
  transfers between devices with their start and end apart: 8, of which 8 were waited for; matrix products, arithmetic and copies ran while one was open for 5% of the time, Pallas kernels for 0%

commit v1 on v0

v1 whole, which is shorter than its diff:
```python
import functools

import jax
import jax.numpy as jnp
from jax import lax
from jax.experimental import pallas as pl
from jax.experimental.pallas import tpu as pltpu
from jax.sharding import PartitionSpec as P

learn_rate = 0.05
hold_rate = 0.9

MESH = pl.DeviceIdType.MESH
LANES = 128
RING = 4
AHEAD = 2
GATHER_LAG = 2


def apply_rule(total, weight, moment, rate):
    mean = total * rate
    state = hold_rate * moment + (1.0 - hold_rate) * mean * mean
    return weight - learn_rate * mean * lax.rsqrt(state + 1e-06), state


def kernel(A, B, K, T, S, rate, *refs):
    grads, weights, moments = refs[:K], refs[K : 2 * K], refs[2 * K : 3 * K]
    small_in = refs[3 * K]
    outs = refs[3 * K + 1 :]
    copies, news, states = outs[:K], outs[K : 2 * K], outs[2 * K : 3 * K]
    small_out = outs[3 * K]
    (acc, rx, rz, wv, mv, out,
     ld_sem, st_sem, cp_sem, xs, xr, rs, ls, zr, gs, gr, hs, ks, hr,
     ns, nr) = outs[3 * K + 1 :]
    C = K * T * S
    R = acc.shape[2]
    n = A * B
    me = lax.axis_index("replica")
    a, b = me // B, me % B

    def dev(row, col):
        return {"replica": row * B + col}

    def send(src, dst, ssem, rsem, to):
        return pltpu.make_async_remote_copy(
            src_ref=src, dst_ref=dst, send_sem=ssem, recv_sem=rsem,
            device_id=to, device_id_type=MESH,
        )

    def valid(c):
        return jnp.logical_and(c >= 0, c < C)

    def rows_cols(c):
        rest = c % (T * S)
        t, u = rest // S, rest % S
        return (pl.ds(pl.multiple_of(u * R, R), R),
                pl.ds(pl.multiple_of(t * LANES, LANES), LANES))

    def for_matrix(c, fn):
        k = c // (T * S)
        rows, cols = rows_cols(c)
        for i in range(K):
            @pl.when(k == i)
            def _(i=i):
                fn(i, rows, cols)

    barrier = pltpu.get_barrier_semaphore()
    for i in range(1, n):
        pl.semaphore_signal(
            barrier, inc=1, device_id={"replica": (me + i) % n}, device_id_type=MESH
        )
    pl.semaphore_wait(barrier, n - 1)

    def x_copy(i, rows, cols, c, j):
        to = (b + j) % B
        return send(
            grads[i].at[:, to, rows, cols], rx.at[c, j - 1],
            xs.at[c % RING, j - 1], xr.at[c, j - 1], dev(a, to),
        )

    def load(i, rows, cols, c):
        q = c % RING
        return (
            pltpu.make_async_copy(grads[i].at[:, b, rows, cols], acc.at[c], ld_sem.at[q, 0]),
            pltpu.make_async_copy(weights[i].at[rows, cols], wv.at[c], ld_sem.at[q, 1]),
            pltpu.make_async_copy(moments[i].at[rows, cols], mv.at[c], ld_sem.at[q, 2]),
        )

    def begin(c):
        @pl.when(c >= RING)
        def _():
            for j in range(1, B):
                x_copy(0, *rows_cols(0), c - RING, j).wait_send()

        def go(i, rows, cols):
            for j in range(1, B):
                x_copy(i, rows, cols, c, j).start()
            for one in load(i, rows, cols, c):
                one.start()

        for_matrix(c, go)

    def add_first(c):
        for one in load(0, *rows_cols(0), c):
            one.wait()
        for j in range(1, B):
            x_copy(0, *rows_cols(0), c, j).wait_recv()
        for d in range(A):
            total = acc[c, d]
            for j in range(1, B):
                total = total + rx[c, j - 1, d]
            acc[c, d] = total

    def r_copy(c, d):
        return send(acc.at[c, d], rz.at[c, d], rs.at[c % RING, d], zr.at[c, d], dev(a + 1, b))

    def l_copy(c, d):
        slot = jnp.where(a - 1 == d, A, d)
        return send(acc.at[c, d], rz.at[c, slot], ls.at[c % RING, d], zr.at[c, slot], dev(a - 1, b))

    def go_right(c):
        for d in range(A):
            @pl.when(jnp.logical_and(d >= a, a > 0))
            def _(d=d):
                r_copy(c, d).wait_recv()

            @pl.when(jnp.logical_and(d > a, a > 0))
            def _(d=d):
                acc[c, d] = acc[c, d] + rz[c, d]

            @pl.when(d > a)
            def _(d=d):
                @pl.when(c >= RING)
                def _():
                    r_copy(c - RING, d).wait_send()

                r_copy(c, d).start()

    def go_left(c):
        @pl.when(a < A - 1)
        def _():
            send(acc.at[c, 0], rz.at[c, A], ls.at[0, 0], zr.at[c, A], dev(a, b)).wait_recv()

        for d in range(A):
            @pl.when(jnp.logical_and(d < a, a < A - 1))
            def _(d=d):
                send(acc.at[c, d], rz.at[c, d], ls.at[0, d], zr.at[c, d], dev(a, b)).wait_recv()
                acc[c, d] = acc[c, d] + rz[c, d]

            @pl.when(d < a)
            def _(d=d):
                @pl.when(c >= RING)
                def _():
                    l_copy(c - RING, d).wait_send()

                l_copy(c, d).start()

    def g_copy(c, j):
        return send(
            out.at[c, a, b], out.at[c, a, b], gs.at[c % RING, j - 1],
            gr.at[c, j - 1], dev(a, (b + j) % B),
        )

    def h_copy(c, o):
        return send(out.at[c, o], out.at[c, o], hs.at[c % RING, o], hr.at[c, o], dev(a + 1, b))

    def k_copy(c, o):
        return send(out.at[c, o], out.at[c, o], ks.at[c % RING, o], hr.at[c, o], dev(a - 1, b))

    def store(i, rows, cols, c):
        q = c % RING
        return (
            pltpu.make_async_copy(wv.at[c], news[i].at[rows, cols], st_sem.at[q, 0]),
            pltpu.make_async_copy(mv.at[c], states[i].at[rows, cols], st_sem.at[q, 1]),
        )

    def update(c):
        @pl.when(a > 0)
        def _():
            acc[c, a] = acc[c, a] + rz[c, a]

        @pl.when(a < A - 1)
        def _():
            acc[c, a] = acc[c, a] + rz[c, A]

        new, state = apply_rule(acc[c, a], wv[c], mv[c], rate)
        wv[c] = new
        mv[c] = state
        out[c, a, b] = new.astype(jnp.bfloat16)

        @pl.when(c >= RING)
        def _():
            for j in range(1, B):
                g_copy(c - RING, j).wait_send()
            for one in store(0, *rows_cols(0), c - RING):
                one.wait()

        for j in range(1, B):
            g_copy(c, j).start()

        def go(i, rows, cols):
            for one in store(i, rows, cols, c):
                one.start()

        for_matrix(c, go)

    def pass_on(c, o, right, left):
        @pl.when(right)
        def _():
            @pl.when(c >= RING)
            def _():
                h_copy(c - RING, o).wait_send()

            h_copy(c, o).start()

        @pl.when(left)
        def _():
            @pl.when(c >= RING)
            def _():
                k_copy(c - RING, o).wait_send()

            k_copy(c, o).start()

    def spread(c):
        for j in range(1, B):
            g_copy(c, j).wait_recv()
        for o in range(A):
            @pl.when(o == a)
            def _(o=o):
                pass_on(c, o, a < A - 1, a > 0)

    def forward(c, o):
        h_copy(c, o).wait_recv()
        pass_on(
            c, o,
            jnp.logical_and(o < a, a < A - 1),
            jnp.logical_and(o > a, a > 0),
        )

    def put(i, rows, cols, c):
        return pltpu.make_async_copy(
            out.at[c], copies[i].at[:, :, rows, cols], cp_sem.at[c % RING]
        )

    def finish(c):
        @pl.when(c >= RING)
        def _():
            put(0, *rows_cols(0), c - RING).wait()

        for_matrix(c, lambda i, rows, cols: put(i, rows, cols, c).start())

    def n_copy(i):
        return send(
            small_in, small_out.at[me], ns.at[i - 1], nr.at[i - 1],
            {"replica": (me + i) % n},
        )

    for c in range(min(AHEAD, C)):
        begin(c)
    for i in range(1, n):
        n_copy(i).start()
    small_out[me] = small_in[...]

    late = (A - 1) + GATHER_LAG

    def step(s, carry):
        def at(c, fn):
            @pl.when(valid(c))
            def _():
                fn(c)

        @pl.when(s + AHEAD < C)
        def _():
            begin(s + AHEAD)

        at(s, add_first)
        at(s - a, go_right)
        at(s - (A - 1 - a), go_left)
        at(s - (A - 1), update)
        at(s - late, spread)
        for o in range(A):
            c = s - late - jnp.abs(a - o)

            @pl.when(jnp.logical_and(valid(c), o != a))
            def _(o=o, c=c):
                forward(c, o)
        at(s - late - (A - 1), finish)
        return carry

    lax.fori_loop(0, C + late + A - 1, step, 0)

    for c in range(max(0, C - RING), C):
        for j in range(1, B):
            x_copy(0, *rows_cols(0), c, j).wait_send()
            g_copy(c, j).wait_send()
        for one in store(0, *rows_cols(0), c):
            one.wait()
        put(0, *rows_cols(0), c).wait()
        for d in range(A):
            @pl.when(d > a)
            def _(d=d, c=c):
                r_copy(c, d).wait_send()

            @pl.when(d < a)
            def _(d=d, c=c):
                l_copy(c, d).wait_send()

            @pl.when(jnp.logical_and(d <= a, a < A - 1))
            def _(d=d, c=c):
                h_copy(c, d).wait_send()

            @pl.when(jnp.logical_and(d >= a, a > 0))
            def _(d=d, c=c):
                k_copy(c, d).wait_send()
    for i in range(1, n):
        n_copy(i).wait()


def exchange(grads, weights, moments, small, n):
    B = max(k for k in range(1, n + 1) if n % k == 0 and k * k <= n)
    A = n // B
    K = len(grads)
    rows, width = weights[0].shape
    T = width // LANES
    S = 1
    R = rows // S
    C = K * T * S
    grads = [g.reshape(A, B, rows, width) for g in grads]
    dma = pltpu.SemaphoreType.DMA
    anywhere = pl.BlockSpec(memory_space=pltpu.MemorySpace.HBM)
    vmem = pl.BlockSpec(memory_space=pltpu.VMEM)
    f32 = jnp.float32
    res = pl.pallas_call(
        functools.partial(kernel, A, B, K, T, S, n ** (-0.5)),
        out_shape=(
            [jax.ShapeDtypeStruct((A, B, rows, width), jnp.bfloat16)] * K
            + [jax.ShapeDtypeStruct((rows, width), f32)] * (2 * K)
            + [jax.ShapeDtypeStruct((n,) + small.shape, f32)]
        ),
        in_specs=[anywhere] * (3 * K) + [vmem],
        out_specs=[anywhere] * (3 * K) + [vmem],
        scratch_shapes=[
            pltpu.VMEM((C, A, R, LANES), f32),
            pltpu.VMEM((C, B - 1, A, R, LANES), f32),
            pltpu.VMEM((C, A + 1, R, LANES), f32),
            pltpu.VMEM((C, R, LANES), f32),
            pltpu.VMEM((C, R, LANES), f32),
            pltpu.VMEM((C, A, B, R, LANES), jnp.bfloat16),
            dma((RING, 3)), dma((RING, 2)), dma((RING,)),
            dma((RING, B - 1)), dma((C, B - 1)),
            dma((RING, A)), dma((RING, A)), dma((C, A + 1)),
            dma((RING, B - 1)), dma((C, B - 1)),
            dma((RING, A)), dma((RING, A)), dma((C, A)),
            dma((n - 1,)), dma((n - 1,)),
        ],
        compiler_params=pltpu.CompilerParams(
            collective_id=0, has_side_effects=True, vmem_limit_bytes=64 * 1000 * 1000
        ),
        name="exchange",
    )(*grads, *weights, *moments, small)
    copies = [c.reshape(n * rows, width) for c in res[:K]]
    return copies, res[K : 2 * K], res[2 * K : 3 * K], res[3 * K]


def per_device(*args):
    grads = [g[0] for g in args[:7]]
    weights, moments = list(args[7:14]), list(args[14:21])
    n = lax.axis_size("replica")

    def three(arrays):
        up, down, query, key, value, mixed = arrays
        return [up, down.T, jnp.concatenate([query, key, value, mixed.T], axis=1)]

    attn = grads[2].shape[1]

    def six(arrays):
        up, down, rest = arrays
        query, key, value, mixed = (rest[:, i * attn : (i + 1) * attn] for i in range(4))
        return [up, down.T, query, key, value, mixed.T]

    total, own = grads[6].shape[0], weights[6].shape[0]
    small = jnp.concatenate([grads[6], weights[6], moments[6]])
    pad = -small.shape[0] % (8 * LANES)
    small = jnp.pad(small, (0, pad)).reshape(-1, LANES)
    copies, news, states, smalls = exchange(
        three(grads[:6]), three(weights[:6]), three(moments[:6]), small, n
    )
    smalls = smalls.reshape(n, -1)
    norm_new, norm_state = apply_rule(
        jnp.sum(smalls[:, :total], axis=0),
        smalls[:, total : total + own].reshape(-1),
        smalls[:, total + own : total + 2 * own].reshape(-1),
        n ** (-0.5),
    )
    start = lax.axis_index("replica") * own
    mine = lambda v: lax.dynamic_slice_in_dim(v, start, own)
    return (
        *six(copies), norm_new.astype(jnp.bfloat16),
        *six(news), mine(norm_new),
        *six(states), mine(norm_state),
    )


def solution(mesh):
    whole = [P(None, "model"), P("model", None)]
    shard = [P("replica", "model"), P("model", "replica")]
    kinds = [0, 1, 0, 0, 0, 1]
    grads = [P("replica", *whole[k]) for k in kinds] + [P("replica", None)]
    shards = [shard[k] for k in kinds] + [P("replica")]
    gathered = [whole[k] for k in kinds] + [P()]
    return jax.shard_map(
        per_device,
        mesh=mesh,
        in_specs=(*grads, *shards, *shards),
        out_specs=(*gathered, *shards, *shards),
        check_vma=False,
    )
```

time: 701 us -> 347 us (0.50)
  waiting for transfers between devices: 463 us -> 0 us
  Pallas kernels: 0 us -> 289 us
  blocking collectives: 180 us -> 0 us
  local copies, waits for them, and re-layouts: 29.9 us -> 56.6 us
  between operations: 15 us -> 0.82 us
  other arithmetic: 13.4 us -> 0.72 us
    reduce_scatter x6 -> x0, waiting for transfers between devices: 368 us -> none  [the longest x1 122 us: per_device(): lax.psum_scatter(grad_down[0].astype(jnp.float32), 'replica', scatter_dim...]
    pallas_call x0 -> x1, Pallas kernels: none -> 289 us  [exchange(): pl.pallas_call(functools.partial(kernel, A, B, K, T, S, n ** (-0.5)), out...]
    all_gather x4 -> x0, blocking collectives: 141 us -> none  [the longest x1 35.6 us: per_device(): lax.all_gather(new_value.astype(jnp.bfloat16), 'replica', axis=0, tiled=T...]
    all_gather x2 -> x0, waiting for transfers between devices: 93.4 us -> none  [the longest x1 62.8 us: per_device(): lax.all_gather(new_down.astype(jnp.bfloat16), 'replica', axis=1, tiled=True)]
    psum x1 -> x0, blocking collectives: 20.7 us -> none  [per_device(): whole_norm = lax.psum(grad_norm[0].astype(jnp.float32), 'replica')]
    unnamed x1 -> x0, blocking collectives: 17.8 us -> none
    transpose x0 -> x3, local copies, waits for them, and re-layouts: none -> 14.4 us  [the longest x2 11.2 us: three(): return [up, down.T, jnp.concatenate([query, key, value, mixed.T], axis=1)]]
    convert_element_type x7 -> x1, other arithmetic: 13.3 us -> 0.61 us  [per_device(): norm_new.astype(jnp.bfloat16)]
  transfers between devices with their start and end apart: 8 -> 0, of which waited for: 8 -> 0; matrix products, arithmetic and copies ran while one was open for 5% -> 0% of each run, Pallas kernels for 0% -> 0%
where the time goes in v1:
time: 347 us
  Pallas kernels  289 us (83%)
  local copies, waits for them, and re-layouts  56.6 us (16%)
    pallas_call x1, Pallas kernels, exchange(): pl.pallas_call(functools.partial(kernel, A, B, K, T, S, n ** (-0.5)), out...  289 us
    unnamed x51, local copies, waits for them, and re-layouts  20.8 us
    transpose x2, local copies, waits for them, and re-layouts, three(): return [up, down.T, jnp.concatenate([query, key, value, mixed.T], axis=1)]  11.2 us
    concatenate x3, local copies, waits for them, and re-layouts, three(): return [up, down.T, jnp.concatenate([query, key, value, mixed.T], axis=1)]  10.6 us

profile of v1, /device:TPU:0, one launch (start us, length us, event | category | flops | bytes accessed | tf_op | source)
XLA Modules:
  0.0 346.7 jit_solution(7263032342507075744)
XLA Ops:
  0.7 1.8 copy.43
  2.5 2.8 copy.44
  5.3 2.8 copy.45
  8.0 2.9 copy.46
  10.9 8.4 %concatenate.25.refs_2_ = f32[4,2,160,1280]{3,2,1,0:T(8,128)} concatenate(f32[4,2,160,320]{3,2,1,0:T(8,128)S(1)} %bitcast.34, f32[4,2,160,320]{3,2,1,0:T(8,128)} %bitcast.35, f32[4,2,160,320]{3,2,1,0:T(8,128)} %bitcast.36, f32[4,2,160,320]{3,2,1,0:T(8,128)} %bitcast.37), dimensions={3} | concatenate | bytes 13107200 | tf_op jit(solution)/shard_map/concatenate | solution.py:372
  19.4 8.3 %copy.42 = f32[1280,1280]{1,0:T(8,128)} copy(f32[1280,1280]{0,1:T(8,128)} %bitcast.38) | data formatting | bytes 13107200 | tf_op jit(solution)/shard_map/transpose | solution.py:372
  27.8 1.1 concatenate.26.refs_5_
  28.9 1.1 concatenate.27.refs_8_
  30.7 288.6 %exchange.1 = (bf16[4,2,160,1280]{3,2,1,0:T(8,128)(2,1)}, bf16[4,2,160,1280]{3,2,1,0:T(8,128)(2,1)}, bf16[4,2,160,1280]{3,2,1,0:T(8,128)(2,1)}, f32[160,1280]{1,...) custom-call(f32[4,2,160,1280]{3,2,1,0:T(8,128)} %bitcast.39, ...), custom_call_target="tpu_custom_call" | custom-call | tf_op jit(solution)/shard_map/exchange/pallas_call | solution.py:333
  319.3 1.0 copy.58
  321.2 0.6 dynamic_slice.6
  321.8 0.6 dynamic_slice.7
  322.5 3.1 slice_bitcast_fusion
  325.6 3.0 fusion.1
  328.6 2.3 copy.55
  330.9 2.2 copy.52
  333.1 1.3 copy.53
  334.4 1.3 copy.54
  335.6 5.8 %copy.47 = bf16[1280,1280]{0,1:T(8,128)(2,1)} copy(bf16[1280,1280]{1,0:T(8,128)(2,1)} %bitcast.42) | data formatting | bytes 6553600 | tf_op jit(solution)/shard_map/reshape | solution.py:361
  341.4 1.7 copy.64
  343.2 0.9 copy.65
  344.1 0.9 copy.66
  344.9 0.9 copy.67
  345.8 0.9 copy.68
  (46 shorter events, 1.6 us)
Async XLA Ops:
  19.4 8.4 %copy-start.8 = (f32[160,320]{1,0:T(8,128)S(1)}, f32[160,320]{1,0:T(8,128)}, u32[]{:S(2)}) copy-start(f32[160,320]{1,0:T(8,128)} %param.30) | copy-start | bytes 614404
  19.4 8.4 %copy-start.9 = (f32[160,320]{1,0:T(8,128)S(1)}, f32[160,320]{1,0:T(8,128)}, u32[]{:S(2)}) copy-start(f32[160,320]{1,0:T(8,128)} %param.31) | copy-start | bytes 614404
  19.4 8.4 %copy-start.10 = (f32[160,320]{1,0:T(8,128)S(1)}, f32[160,320]{1,0:T(8,128)}, u32[]{:S(2)}) copy-start(f32[160,320]{1,0:T(8,128)} %param.32) | copy-start | bytes 614404
  19.4 8.4 %copy-start.11 = (f32[320,160]{0,1:T(8,128)S(1)}, f32[320,160]{0,1:T(8,128)}, u32[]{:S(2)}) copy-start(f32[320,160]{0,1:T(8,128)} %param.33) | copy-start | bytes 614404
  19.4 9.5 %copy-start.12 = (f32[160,320]{1,0:T(8,128)S(1)}, f32[160,320]{1,0:T(8,128)}, u32[]{:S(2)}) copy-start(f32[160,320]{1,0:T(8,128)} %param.37) | copy-start | bytes 614404
  19.4 9.5 %copy-start.13 = (f32[160,320]{1,0:T(8,128)S(1)}, f32[160,320]{1,0:T(8,128)}, u32[]{:S(2)}) copy-start(f32[160,320]{1,0:T(8,128)} %param.38) | copy-start | bytes 614404
  19.4 9.5 %copy-start.14 = (f32[160,320]{1,0:T(8,128)S(1)}, f32[160,320]{1,0:T(8,128)}, u32[]{:S(2)}) copy-start(f32[160,320]{1,0:T(8,128)} %param.39) | copy-start | bytes 614404
  19.4 9.5 %copy-start.15 = (f32[320,160]{0,1:T(8,128)S(1)}, f32[320,160]{0,1:T(8,128)}, u32[]{:S(2)}) copy-start(f32[320,160]{0,1:T(8,128)} %param.40) | copy-start | bytes 614404
  27.8 2.2 copy-start.16
  27.8 2.3 copy-start.17
  27.8 2.3 copy-start.18
  319.3 6.3 %copy-start = (bf16[4,2,160,1280]{3,2,1,0:T(8,128)(2,1)S(1)}, bf16[4,2,160,1280]{3,2,1,0:T(8,128)(2,1)}, u32[]{:S(2)}) copy-start(bf16[4,2,160,1280]{3,2,1,0:T(8,128)(2,1)} %get-tuple-element.33) | copy-start | bytes 9830404
  328.6 4.5 %copy-start.2 = (bf16[1280,320]{1,0:T(8,128)(2,1)S(1)}, bf16[1280,320]{1,0:T(8,128)(2,1)}, u32[]{:S(2)}) copy-start(bf16[1280,320]{1,0:T(8,128)(2,1)} %get-tuple-element.45) | copy-start | bytes 2457604
  328.6 5.8 %copy-start.1 = (bf16[1280,320]{1,0:T(8,128)(2,1)S(1)}, bf16[1280,320]{1,0:T(8,128)(2,1)}, u32[]{:S(2)}) copy-start(bf16[1280,320]{1,0:T(8,128)(2,1)} %get-tuple-element.44) | copy-start | bytes 2457604
  335.6 5.8 %copy-start.3 = (bf16[4,2,160,1280]{3,2,1,0:T(8,128)(2,1)S(1)}, bf16[4,2,160,1280]{3,2,1,0:T(8,128)(2,1)}, u32[]{:S(2)}) copy-start(bf16[4,2,160,1280]{3,2,1,0:T(8,128)(2,1)} %get-tuple-element.31) | copy-start | bytes 9830404
  341.4 1.7 copy-start.7
  341.4 2.6 copy-start.6
  341.4 3.5 %copy-start.5 = (f32[160,1280]{1,0:T(8,128)S(1)}, f32[160,1280]{1,0:T(8,128)}, u32[]{:S(2)}) copy-start(f32[160,1280]{1,0:T(8,128)} %get-tuple-element.97) | copy-start | bytes 2457604
  343.2 2.7 copy-start.4
